TPU v7x, 256 devices: a whole 4x4x8 slice. The times are simulated.
256 devices in a mesh: row: 16 (over z, y_hi), col: 8 (over x, core), depth: 2 (over y_lo).
Axes of the slice: x: 4, y: 4 (y_hi: 2, y_lo: 2; y = y_hi * 2 + y_lo), z: 8, core: 2. Of those that a mesh axis runs over, the one named last changes fastest.
Arguments:
- heads_concat: bfloat16 [8192, 16384], P('row', ('depth', 'col')), may hold values from -6 to 6
- w_out: bfloat16 [16384, 7168], P(('depth', 'row'), 'col'), may hold values from -0.046875 to 0.046875
Outputs:
- projected: bfloat16 [8192, 7168], P('row', ('col', 'depth'))
All inputs are finite; a program needn't handle non-finite values.
Results may differ from a plain program's by a relative error of at most 0.001.
Values may be sent and summed in bfloat16 or wider, within the bound.
A program may use at most 128 MiB of HBM per device.

v0:
```python
import jax
import jax.numpy as jnp
from jax import lax
from jax.sharding import PartitionSpec as P


def from_everyone(array, axis):
    copies = jnp.broadcast_to(array, (lax.axis_size(axis), *array.shape))
    return lax.all_to_all(copies, axis, split_axis=0, concat_axis=0, tiled=True)


def joined_along(tiles, dim):
    tiles = jnp.moveaxis(tiles, 0, dim)
    shape = tiles.shape
    return tiles.reshape(*shape[:dim], shape[dim] * shape[dim + 1], *shape[dim + 2 :])


def collect(array, axis, dim):
    tiles = from_everyone(array, axis)
    return joined_along(tiles, dim)


def in_blocks(array, dim, size):
    shape = array.shape
    tiles = array.reshape(*shape[:dim], size, shape[dim] // size, *shape[dim + 1 :])
    return jnp.moveaxis(tiles, dim, 0)


def summed_on_arrival(array, axis, dim):
    size = lax.axis_size(axis)
    tiles = lax.all_to_all(in_blocks(array, dim, size), axis, 0, 0, tiled=True)
    return jnp.sum(tiles, axis=0)


def per_device(heads_concat, w_out):
    weight_half = lax.all_gather(w_out, "row", axis=0, tiled=True)
    partial_sum = jnp.dot(
        collect(heads_concat, "col", 1), weight_half, preferred_element_type=jnp.float32
    )
    summed = summed_on_arrival(partial_sum, "depth", 1)
    return summed.astype(jnp.bfloat16)


def solution(mesh):
    return jax.shard_map(
        per_device,
        mesh=mesh,
        in_specs=(P("row", ("depth", "col")), P(("depth", "row"), "col")),
        out_specs=P("row", ("col", "depth")),
        check_vma=False,
    )
```

profile of v0, /device:TPU:2, one launch (start us, length us, event | category | flops | bytes accessed | tf_op | source)
XLA Modules:
  0.0 278.8 jit_solution(3857132418449797120)
XLA Ops:
  6.5 0.0 all-gather.2.cloned.1.call-start
  6.5 0.7 all-gather.2.cloned.1.call-update
  7.3 2.3 broadcast_in_dim.3
  9.5 100.0 %all_to_all.10 = bf16[8,512,1024]{2,1,0:T(8,128)(2,1)} all-to-all(bf16[8,512,1024]{2,1,0:T(8,128)(2,1)S(1)} %broadcast_in_dim.3), channel_id=1, replica_groups=mesh['row'=16,'col'=8,'depth'=2] {'col'}, dimensions={0} | all-to-all | bytes 16777216 | tf_op jit(solution)/shard_map/all_to_all | solution.py:9
  109.5 11.4 %copy.4 = bf16[512,8,1024]{2,1,0:T(8,128)(2,1)} copy(bf16[512,8,1024]{2,0,1:T(8,128)(2,1)} %bitcast.7) | data formatting | bytes 16777216 | tf_op jit(solution)/shard_map/transpose | solution.py:13
  120.9 13.5 %reshape.6 = bf16[512,8192,1]{1,0,2:T(8,128)(2,1)} reshape(bf16[512,8,1024]{2,1,0:T(8,128)(2,1)} %copy.4) | data formatting | bytes 16777216 | tf_op jit(solution)/shard_map/reshape | solution.py:15
  134.4 79.6 %all-gather.2.cloned.1.call-done = bf16[8192,896]{1,0:T(8,128)(2,1)} async-done(((bf16[512,896]{1,0:T(8,128)(2,1)}), bf16[8192,896]{1,0:T(8,128)(2,1)}) %all-gather.2.cloned.1.call-update) | async-done | bytes 14680080 | tf_op jit(solution)/shard_map/all_gather | solution.py:36
  214.0 19.4 %copy.5 = bf16[896,8192]{1,0:T(8,128)(2,1)} copy(bf16[896,8192]{0,1:T(8,128)(2,1)} %bitcast.8) | data formatting | bytes 29360128 | tf_op jit(solution)/shard_map/dot_general | solution.py:37
  233.4 13.5 %convolution_bitcast_fusion = f32[2,512,448]{1,2,0:T(8,128)S(1)} fusion(bf16[512,8192,1]{1,0,2:T(8,128)(2,1)} %reshape.6, bf16[2,448,8192]{2,1,0:T(8,128)(2,1)} %bitcast.9), kind=kOutput, calls=%fused_computation | convolution fusion | flops 7516192768 | bytes 24903680 | tf_op jit(solution)/shard_map/dot_general | solution.py:37
  246.9 24.1 %all_to_all.11 = f32[2,512,448]{1,2,0:T(8,128)S(1)} all-to-all(f32[2,512,448]{1,2,0:T(8,128)S(1)} %convolution_bitcast_fusion), channel_id=1, replica_groups=mesh['row'=16,'col'=8,'depth'=2] {'depth'}, dimensions={0} | all-to-all | bytes 3670016 | tf_op jit(solution)/shard_map/all_to_all | solution.py:31
  271.0 1.0 reduce_sum.9
Async XLA Ops:
  6.5 207.5 %all-gather.2.cloned.1.call-start = ((), (), s32[]{:S(2)}) async-start(), calls=%async_computation.2 | async-start | bytes 15597568 | tf_op jit(solution)/shard_map/all_gather | solution.py:36
Sparse Core Ops, SparseCore 0:
  9.9 204.0 all-gather.1
where the time goes:
time: 280 us; the launch traced here: 279 us
  blocking collectives  124 us (44%)
  waiting for transfers between devices  80.3 us (29%)
  local copies, waits for them, and re-layouts  46.5 us (17%)
  matrix products  13.5 us (5%)
  between operations  13.4 us (5%)
    all_to_all x1, blocking collectives, from_everyone(): return lax.all_to_all(copies, axis, split_axis=0, concat_axis=0, tiled=True)  100 us
    all_gather x1, waiting for transfers between devices, per_device(): weight_half = lax.all_gather(w_out, 'row', axis=0, tiled=True)  79.6 us
    all_to_all x1, blocking collectives, summed_on_arrival(): tiles = lax.all_to_all(in_blocks(array, dim, size), axis, 0, 0, tiled=True)  24.1 us
    dot_general x1, local copies, waits for them, and re-layouts, per_device(): jnp.dot(collect(heads_concat, 'col', 1), weight_half, preferred_element_t...  19.4 us
    reshape x1, local copies, waits for them, and re-layouts, joined_along(): tiles.reshape(*shape[:dim], shape[dim] * shape[dim + 1], *shape[dim + 2:])  13.5 us
    dot_general x1, matrix products, per_device(): jnp.dot(collect(heads_concat, 'col', 1), weight_half, preferred_element_t...  13.5 us
    transpose x1, local copies, waits for them, and re-layouts, joined_along(): tiles = jnp.moveaxis(tiles, 0, dim)  11.4 us
  transfers between devices with their start and end apart: 1, of which 1 were waited for; matrix products, arithmetic and copies ran while one was open for 10% of the time, Pallas kernels for 0%

commit v1 on v0

--- a/solution.py
+++ b/solution.py
@@ -33,7 +33,9 @@
 
 
 def per_device(heads_concat, w_out):
-    weight_half = lax.all_gather(w_out, "row", axis=0, tiled=True)
+    weight_half = jnp.concatenate(
+        lax.all_to_all(jnp.stack([w_out] * lax.axis_size("row")), "row", 0, 0), axis=0
+    )
     partial_sum = jnp.dot(
         collect(heads_concat, "col", 1), weight_half, preferred_element_type=jnp.float32
     )

time: 280 us -> 537 us (1.92)
  waiting for transfers between devices: 80.3 us -> 402 us
  blocking collectives: 124 us -> 23.7 us
  local copies, waits for them, and re-layouts: 46.5 us -> 76.8 us
  starting transfers between devices: 0.01 us -> 16.8 us
  between operations: 13.4 us -> 0.03 us
    all_to_all x0 -> x2, waiting for transfers between devices: none -> 402 us  [the longest x1 310 us: per_device(): lax.all_to_all(jnp.stack([w_out] * lax.axis_size('row')), 'row', 0, 0)]
    all_to_all x1 -> x0, blocking collectives: 100 us -> none  [from_everyone(): return lax.all_to_all(copies, axis, split_axis=0, concat_axis=0, tiled=True)]
    all_gather x1 -> x0, waiting for transfers between devices: 79.6 us -> none  [per_device(): weight_half = lax.all_gather(w_out, 'row', axis=0, tiled=True)]
    all_to_all x0 -> x1, local copies, waits for them, and re-layouts: none -> 19.9 us  [per_device(): lax.all_to_all(jnp.stack([w_out] * lax.axis_size('row')), 'row', 0, 0)]
    all_to_all x0 -> x2, starting transfers between devices: none -> 16.8 us  [the longest x1 9.54 us: per_device(): lax.all_to_all(jnp.stack([w_out] * lax.axis_size('row')), 'row', 0, 0)]
    another operation x0 -> x1, local copies, waits for them, and re-layouts: none -> 6.6 us  [per_device(): jnp.stack([w_out] * lax.axis_size('row'))]
  transfers between devices with their start and end apart: 1 -> 2, of which waited for: 1 -> 2; matrix products, arithmetic and copies ran while one was open for 10% -> 5% of each run, Pallas kernels for 0% -> 0%
where the time goes in v1:
time: 537 us; the launch traced here: 534 us
  waiting for transfers between devices  402 us (75%)
  local copies, waits for them, and re-layouts  76.8 us (14%)
  blocking collectives  23.7 us (4%)
  starting transfers between devices  16.8 us (3%)
  matrix products  13.5 us (3%)
    all_to_all x1, waiting for transfers between devices, per_device(): lax.all_to_all(jnp.stack([w_out] * lax.axis_size('row')), 'row', 0, 0)  310 us
    all_to_all x1, waiting for transfers between devices, from_everyone(): return lax.all_to_all(copies, axis, split_axis=0, concat_axis=0, tiled=True)  92.7 us
    all_to_all x1, blocking collectives, summed_on_arrival(): tiles = lax.all_to_all(in_blocks(array, dim, size), axis, 0, 0, tiled=True)  23.7 us
    all_to_all x1, local copies, waits for them, and re-layouts, per_device(): lax.all_to_all(jnp.stack([w_out] * lax.axis_size('row')), 'row', 0, 0)  19.9 us
    dot_general x1, local copies, waits for them, and re-layouts, per_device(): jnp.dot(collect(heads_concat, 'col', 1), weight_half, preferred_element_t...  19.4 us
    reshape x1, local copies, waits for them, and re-layouts, joined_along(): tiles.reshape(*shape[:dim], shape[dim] * shape[dim + 1], *shape[dim + 2:])  13.5 us
    dot_general x1, matrix products, per_device(): jnp.dot(collect(heads_concat, 'col', 1), weight_half, preferred_element_t...  13.5 us
    transpose x1, local copies, waits for them, and re-layouts, joined_along(): tiles = jnp.moveaxis(tiles, 0, dim)  11.3 us
  transfers between devices with their start and end apart: 2, of which 2 were waited for; matrix products, arithmetic and copies ran while one was open for 5% of the time, Pallas kernels for 0%

profile of v1, /device:TPU:2, one launch (start us, length us, event | category | flops | bytes accessed | tf_op | source)
XLA Modules:
  0.0 534.2 jit_solution(7700244152493029967)
XLA Ops:
  0.0 5.5 %broadcast_in_dim.3 = bf16[8,512,1024]{2,1,0:T(8,128)(2,1)} broadcast(bf16[512,1024]{1,0:T(8,128)(2,1)} %param.2), dimensions={1,2} | broadcast | bytes 9437184 | tf_op jit(solution)/shard_map/broadcast_in_dim | solution.py:8
  5.5 0.0 copy-start
  5.5 7.3 %all-to-all-start = ((bf16[8,512,1024]{2,1,0:T(8,128)(2,1)}), bf16[8,512,1024]{2,1,0:T(8,128)(2,1)}, u32[]{:S(2)}, u32[]{:S(2)}) async-start(bf16[8,512,1024]{2,1,0:T(8,128)(2,1)} %broadcast_in_dim.3), calls=%async_computation | async-start | bytes 16777216 | tf_op jit(solution)/shard_map/all_to_all | solution.py:9
  12.8 0.0 copy-done
  12.8 0.5 copy.7
  13.3 92.7 %all-to-all-done = bf16[8,512,1024]{2,1,0:T(8,128)(2,1)} async-done(((bf16[8,512,1024]{2,1,0:T(8,128)(2,1)}), bf16[8,512,1024]{2,1,0:T(8,128)(2,1)}, u32[]{:S(2)}, u32[]{:S(2)}) %all-to-all-start) | async-done | bytes 8388640 | tf_op jit(solution)/shard_map/all_to_all | solution.py:9
  106.1 6.6 %stack.2 = bf16[16,512,896]{1,2,0:T(8,128)(2,1)} broadcast(bf16[512,896]{0,1:T(8,128)(2,1)S(1)} %copy.7), dimensions={1,2} | broadcast | bytes 15597568 | tf_op jit(solution)/shard_map/stack | solution.py:37
  112.7 9.5 %all-to-all-start.1 = ((bf16[16,512,896]{1,2,0:T(8,128)(2,1)}), bf16[16,512,896]{1,2,0:T(8,128)(2,1)}, u32[]{:S(2)}, u32[]{:S(2)}) async-start(bf16[16,512,896]{1,2,0:T(8,128)(2,1)} %stack.2), calls=%async_computation.1 | async-start | bytes 29360128 | tf_op jit(solution)/shard_map/all_to_all | solution.py:37
  122.2 11.3 %copy.6 = bf16[512,8,1024]{2,1,0:T(8,128)(2,1)} copy(bf16[512,8,1024]{2,0,1:T(8,128)(2,1)} %bitcast) | data formatting | bytes 16777216 | tf_op jit(solution)/shard_map/transpose | solution.py:13
  133.5 13.5 %reshape.12 = bf16[512,8192,1]{1,0,2:T(8,128)(2,1)} reshape(bf16[512,8,1024]{2,1,0:T(8,128)(2,1)} %copy.6) | data formatting | bytes 16777216 | tf_op jit(solution)/shard_map/reshape | solution.py:15
  147.0 309.8 %all-to-all-done.1 = bf16[16,512,896]{1,2,0:T(8,128)(2,1)} async-done(((bf16[16,512,896]{1,2,0:T(8,128)(2,1)}), bf16[16,512,896]{1,2,0:T(8,128)(2,1)}, u32[]{:S(2)}, u32[]{:S(2)}) %all-to-all-start.1) | async-done | bytes 14680096 | tf_op jit(solution)/shard_map/all_to_all | solution.py:37
  456.7 19.9 %copy.8 = bf16[16,512,896]{2,1,0:T(8,128)(2,1)} copy(bf16[16,512,896]{1,2,0:T(8,128)(2,1)} %all-to-all-done.1) | data formatting | bytes 29360128 | tf_op jit(solution)/shard_map/all_to_all | solution.py:37
  476.6 19.4 %copy.9 = bf16[896,8192]{1,0:T(8,128)(2,1)} copy(bf16[896,8192]{0,1:T(8,128)(2,1)} %bitcast.9) | data formatting | bytes 29360128 | tf_op jit(solution)/shard_map/dot_general | solution.py:39
  496.1 13.5 %convolution_bitcast_fusion = f32[2,512,448]{1,2,0:T(8,128)S(1)} fusion(bf16[512,8192,1]{1,0,2:T(8,128)(2,1)} %reshape.12, bf16[2,448,8192]{2,1,0:T(8,128)(2,1)} %bitcast.10), kind=kOutput, calls=%fused_computation | convolution fusion | flops 7516192768 | bytes 24903680 | tf_op jit(solution)/shard_map/dot_general | solution.py:39
  509.5 23.7 %all_to_all.15 = f32[2,512,448]{1,2,0:T(8,128)S(1)} all-to-all(f32[2,512,448]{1,2,0:T(8,128)S(1)} %convolution_bitcast_fusion), channel_id=1, replica_groups=mesh['row'=16,'col'=8,'depth'=2] {'depth'}, dimensions={0} | all-to-all | bytes 3670016 | tf_op jit(solution)/shard_map/all_to_all | solution.py:31
  533.2 1.0 reduce_sum.9
Async XLA Ops:
  5.5 7.3 %copy-start = (bf16[512,896]{1,0:T(8,128)(2,1)S(1)}, bf16[512,896]{1,0:T(8,128)(2,1)}, u32[]{:S(2)}) copy-start(bf16[512,896]{1,0:T(8,128)(2,1)} %param.3) | copy-start | bytes 2752516
  5.5 100.5 %all-to-all-start = ((bf16[8,512,1024]{2,1,0:T(8,128)(2,1)}), bf16[8,512,1024]{2,1,0:T(8,128)(2,1)}, u32[]{:S(2)}, u32[]{:S(2)}) async-start(bf16[8,512,1024]{2,1,0:T(8,128)(2,1)} %broadcast_in_dim.3), calls=%async_computation | async-start | bytes 16777216 | tf_op jit(solution)/shard_map/all_to_all | solution.py:9
  112.7 344.1 %all-to-all-start.1 = ((bf16[16,512,896]{1,2,0:T(8,128)(2,1)}), bf16[16,512,896]{1,2,0:T(8,128)(2,1)}, u32[]{:S(2)}, u32[]{:S(2)}) async-start(bf16[16,512,896]{1,2,0:T(8,128)(2,1)} %stack.2), calls=%async_computation.1 | async-start | bytes 29360128 | tf_op jit(solution)/shard_map/all_to_all | solution.py:37
